TPU v7x, 32 devices: a whole 2x2x4 slice. The times are simulated.
32 devices in a mesh: rep: 8 (over y, x, core), tp: 4 (over z).
Axes of the slice: x: 2, y: 2, z: 4, core: 2. Of those that a mesh axis runs over, the one named last changes fastest.
Arguments:
- tokens: bfloat16 [8192, 1280], P(('rep', 'tp')), may hold values from -6 to 6
- view_ids: int32 [32, 4], P('rep'), may hold values from 0 to 31
- time_ids: int32 [32], P('rep'), may hold values from 0 to 999
- camera_table: float32 [32, 1280], replicated, may hold values from -6 to 6
- norm_attn: float32 [2, 1280], replicated, may hold values from 0.1 to 1.9
- norm_ffn: float32 [2, 1280], replicated, may hold values from 0.1 to 1.9
- w_query: bfloat16 [2, 1280, 1280], P(None, ('rep', 'tp')), may hold values from -0.1677051 to 0.1677051
- w_key: bfloat16 [2, 1280, 1280], P(None, ('rep', 'tp')), may hold values from -6.764106 to 6.764106
- w_value: bfloat16 [2, 1280, 1280], P(None, ('rep', 'tp')), may hold values from -0.15625 to 0.15625
- w_out: bfloat16 [2, 1280, 1280], P(None, ('rep', 'tp')), may hold values from -0.15625 to 0.15625
- w_gate: bfloat16 [2, 1280, 5120], P(None, ('rep', 'tp')), may hold values from -0.15625 to 0.15625
- w_up: bfloat16 [2, 1280, 5120], P(None, ('rep', 'tp')), may hold values from -0.15625 to 0.15625
- w_down: bfloat16 [2, 1280, 5120], P(None, ('rep', 'tp')), may hold values from -0.078125 to 0.078125
Outputs:
- denoised: bfloat16 [8192, 1280], P(('rep', 'tp'))
All inputs are finite; a program needn't handle non-finite values.
Results may differ from a plain program's by a relative error of at most 0.035.
Values may be sent and summed in bfloat16 or wider, within the bound.
A program may use at most 128 MiB of HBM per device.

v0:
```python
import math
import jax
import jax.numpy as jnp
from jax import lax
from jax.sharding import PartitionSpec as P

D = 1280
HEADS = 8
VIEWS = 4
HW = 64
LAYERS = 2


def layer_norm(activations, gain_vector):
    average = jnp.mean(activations, axis=-1, keepdims=True)
    centred = activations - average
    spread = jnp.mean(centred * centred, axis=-1, keepdims=True)
    return (centred * lax.rsqrt(spread + 1e-05) * gain_vector).astype(jnp.bfloat16)


def time_code(step_ids, width):
    half_width = width // 2
    frequency = jnp.exp(-math.log(10000.0) * jnp.arange(half_width, dtype=jnp.float32) / half_width)
    angles = step_ids.astype(jnp.float32)[:, None] * frequency[None, :]
    return jnp.concatenate([jnp.cos(angles), jnp.sin(angles)], axis=1)


def conditioning(row_ids, view_ids, time_ids, camera_table):
    set_ids = row_ids // (VIEWS * HW)
    slot_ids = set_ids * VIEWS + row_ids // HW % VIEWS
    flat_views = view_ids.reshape(-1)
    slot_range = jnp.arange(flat_views.shape[0], dtype=jnp.int32)
    pose_ids = jnp.sum(
        jnp.where(slot_ids[:, None] == slot_range[None, :], flat_views[None, :], 0), axis=1
    )
    set_range = jnp.arange(time_ids.shape[0], dtype=jnp.int32)
    step_ids = jnp.sum(
        jnp.where(set_ids[:, None] == set_range[None, :], time_ids[None, :], 0), axis=1
    )
    pose_range = jnp.arange(camera_table.shape[0], dtype=jnp.int32)
    onehot_pose = (pose_ids[:, None] == pose_range[None, :]).astype(jnp.float32)
    camera = jnp.dot(onehot_pose, camera_table, precision=lax.Precision.HIGHEST)
    return camera + time_code(step_ids, camera_table.shape[1])


def reshard(weights):
    owned = (
        lax.all_to_all(weights[0], "tp", split_axis=2, concat_axis=1, tiled=True),
        lax.all_to_all(weights[1], "tp", split_axis=2, concat_axis=1, tiled=True),
        lax.all_to_all(weights[2], "tp", split_axis=2, concat_axis=1, tiled=True),
        lax.all_to_all(weights[3], "tp", split_axis=2, concat_axis=1, tiled=True),
        lax.all_to_all(weights[4], "tp", split_axis=2, concat_axis=1, tiled=True),
        lax.all_to_all(weights[5], "tp", split_axis=2, concat_axis=1, tiled=True),
        lax.all_to_all(weights[6], "tp", split_axis=2, concat_axis=1, tiled=True),
    )
    return (
        lax.all_gather(owned[0], "rep", axis=1, tiled=True),
        lax.all_gather(owned[1], "rep", axis=1, tiled=True),
        lax.all_gather(owned[2], "rep", axis=1, tiled=True),
        lax.all_gather(owned[3], "rep", axis=1, tiled=True),
        lax.all_gather(owned[4], "rep", axis=1, tiled=True),
        lax.all_gather(owned[5], "rep", axis=1, tiled=True),
        lax.all_gather(owned[6], "rep", axis=1, tiled=True),
    )


def attend(packed, width_local, head_size):
    total_rows = packed.shape[0]
    set_count = total_rows // (VIEWS * HW)
    heads_here = width_local // head_size
    shape_heads = (set_count, VIEWS * HW, heads_here, head_size)
    query_rows = packed[:, :width_local].reshape(shape_heads)
    key_rows = packed[:, width_local : 2 * width_local].reshape(shape_heads)
    value_rows = packed[:, 2 * width_local :].reshape(shape_heads)
    scores = jnp.einsum(
        "bqhd,bkhd->bhqk", query_rows, key_rows, preferred_element_type=jnp.float32
    ) * head_size ** (-0.5)
    peak = jnp.max(scores, axis=-1, keepdims=True)
    expons = jnp.exp(scores - peak)
    attn_probs = (expons / jnp.sum(expons, axis=-1, keepdims=True)).astype(jnp.bfloat16)
    mixed_rows = jnp.einsum(
        "bhqk,bkhd->bqhd", attn_probs, value_rows, preferred_element_type=jnp.float32
    )
    return mixed_rows.astype(jnp.bfloat16).reshape(total_rows, width_local)


def out_terms(mixed_rows, weight):
    return lax.dot_general(
        mixed_rows, weight, (((1,), (1,)), ((), ())), preferred_element_type=jnp.float32
    )


def body(
    tokens,
    view_ids,
    time_ids,
    camera_table,
    norm_attn,
    norm_ffn,
    w_query,
    w_key,
    w_value,
    w_out,
    w_gate,
    w_up,
    w_down,
):
    tp_count = lax.axis_size("tp")
    query_w, key_w, value_w, out_w, gate_w, up_w, down_w = reshard(
        (w_query, w_key, w_value, w_out, w_gate, w_up, w_down)
    )
    width_local = query_w.shape[2]
    head_size = D // HEADS
    share_rows = tokens.shape[0]
    group_total = share_rows * tp_count
    first_row = lax.axis_index("tp") * share_rows
    whole_rows = lax.all_gather(tokens, "tp", axis=0, tiled=True)
    row_ids = jnp.arange(group_total, dtype=jnp.int32)
    stream = whole_rows.astype(jnp.float32) + conditioning(
        row_ids, view_ids, time_ids, camera_table
    )

    def total_terms(partial_value):
        return lax.psum(partial_value.astype(jnp.bfloat16), "tp").astype(jnp.float32)

    for layer_index in range(LAYERS):
        query_here = query_w[layer_index]
        key_here = key_w[layer_index]
        value_here = value_w[layer_index]
        gate_here = gate_w[layer_index]
        up_here = up_w[layer_index]
        normed = layer_norm(stream, norm_attn[layer_index])
        packed = jnp.concatenate(
            [
                jnp.dot(normed, query_here, preferred_element_type=jnp.float32).astype(
                    jnp.bfloat16
                ),
                jnp.dot(normed, key_here, preferred_element_type=jnp.float32).astype(jnp.bfloat16),
                jnp.dot(normed, value_here, preferred_element_type=jnp.float32).astype(
                    jnp.bfloat16
                ),
            ],
            axis=1,
        )
        mixed_rows = attend(packed, width_local, head_size)
        stream = stream + total_terms(out_terms(mixed_rows, out_w[layer_index]))
        normed = layer_norm(stream, norm_ffn[layer_index])
        gate_part = jnp.dot(normed, gate_here, preferred_element_type=jnp.float32)
        up_part = jnp.dot(normed, up_here, preferred_element_type=jnp.float32)
        hidden = (jax.nn.gelu(gate_part, approximate=False) * up_part).astype(jnp.bfloat16)
        stream = stream + total_terms(out_terms(hidden, down_w[layer_index]))
    return lax.dynamic_slice_in_dim(stream, first_row, share_rows, 0).astype(jnp.bfloat16)


def solution(mesh):
    return jax.shard_map(
        body,
        mesh=mesh,
        in_specs=(
            P(("rep", "tp"), None),
            P("rep", None),
            P("rep"),
            P(),
            P(),
            P(),
            P(None, ("rep", "tp"), None),
            P(None, ("rep", "tp"), None),
            P(None, ("rep", "tp"), None),
            P(None, ("rep", "tp"), None),
            P(None, ("rep", "tp"), None),
            P(None, ("rep", "tp"), None),
            P(None, ("rep", "tp"), None),
        ),
        out_specs=P(("rep", "tp"), None),
        check_vma=False,
    )
```

profile of v0, /device:TPU:0, one launch (start us, length us, event | category | flops | bytes accessed | tf_op | source)
XLA Modules:
  0.0 892.5 jit_solution(10918619393631502398)
XLA Ops:
  9.8 13.8 %all_to_all.126 = bf16[4,2,12800]{2,1,0:T(2,128)(2,1)S(1)} all-to-all(bf16[4,2,12800]{2,1,0:T(2,128)(2,1)S(1)} %reshape.139), channel_id=1, replica_groups=mesh['rep'=8,'tp'=4] {'tp'}, dimensions={0} | all-to-all | bytes 409600 | tf_op jit(solution)/shard_map/all_to_all | solution.py:48
  27.8 19.7 %all_to_all.127 = bf16[4,2,12800]{2,1,0:T(2,128)(2,1)S(1)} all-to-all(bf16[4,2,12800]{2,1,0:T(2,128)(2,1)S(1)} %reshape.137), channel_id=1, replica_groups=mesh['rep'=8,'tp'=4] {'tp'}, dimensions={0} | all-to-all | bytes 409600 | tf_op jit(solution)/shard_map/all_to_all | solution.py:49
  51.7 14.9 %all_to_all.128 = bf16[4,2,12800]{2,1,0:T(2,128)(2,1)S(1)} all-to-all(bf16[4,2,12800]{2,1,0:T(2,128)(2,1)S(1)} %reshape.141), channel_id=1, replica_groups=mesh['rep'=8,'tp'=4] {'tp'}, dimensions={0} | all-to-all | bytes 409600 | tf_op jit(solution)/shard_map/all_to_all | solution.py:50
  75.7 10.5 %multiply_cosine_fusion = (f32[1024,640]{1,0:T(8,128)S(1)}, f32[1024,640]{1,0:T(8,128)}) fusion(f32[640]{0:T(1024)S(1)} %multiply_exponential_fusion, f32[1024]{0:T(1024)S(1)} %convert_element_type.93), kind=kLoop, calls=%fused_computation.60 | loop fusion | flops 655360 | bytes 5249536 | tf_op jit(solution)/shard_map/cos | solution.py:25
  91.8 5.1 fusion.139
  100.0 4.8 all-gather.13.cloned.1.call-done
  109.7 24.3 %all-gather.15.cloned.1.call-done = bf16[2,1280,320]{2,1,0:T(8,128)(2,1)} async-done(((bf16[2,160,320]{2,1,0:T(8,128)(2,1)}), bf16[2,1280,320]{2,1,0:T(8,128)(2,1)}) %all-gather.15.cloned.1.call-update) | async-done | bytes 1638416 | tf_op jit(solution)/shard_map/all_gather | solution.py:58
  139.5 23.4 %all-gather.11.cloned.1.call-done = bf16[2,1280,320]{2,1,0:T(8,128)(2,1)} async-done(((bf16[2,160,320]{2,1,0:T(8,128)(2,1)}), bf16[2,1280,320]{2,1,0:T(8,128)(2,1)}) %all-gather.11.cloned.1.call-update) | async-done | bytes 1638416 | tf_op jit(solution)/shard_map/all_gather | solution.py:59
  173.8 18.1 %all-gather.17.cloned.1.call-done = bf16[2,1280,320]{2,1,0:T(8,128)(2,1)} async-done(((bf16[2,160,320]{2,1,0:T(8,128)(2,1)}), bf16[2,1280,320]{2,1,0:T(8,128)(2,1)}) %all-gather.17.cloned.1.call-update) | async-done | bytes 1638416 | tf_op jit(solution)/shard_map/all_gather | solution.py:60
  192.0 4.3 convolution_convert_fusion.3
  196.6 4.7 copy.97
  201.3 5.1 reshape.145
  206.4 47.9 %all_to_all.129 = bf16[4,2,51200]{2,1,0:T(2,128)(2,1)} all-to-all(bf16[4,2,51200]{2,1,0:T(2,128)(2,1)} %reshape.145), channel_id=1, replica_groups=mesh['rep'=8,'tp'=4] {'tp'}, dimensions={0} | all-to-all | bytes 1638400 | tf_op jit(solution)/shard_map/all_to_all | solution.py:52
  254.2 5.0 reshape.146
  259.3 4.3 copy.117
  265.8 4.7 copy.100
  270.6 5.1 reshape.147
  275.6 47.5 %all_to_all.130 = bf16[4,2,51200]{2,1,0:T(2,128)(2,1)} all-to-all(bf16[4,2,51200]{2,1,0:T(2,128)(2,1)} %reshape.147), channel_id=1, replica_groups=mesh['rep'=8,'tp'=4] {'tp'}, dimensions={0} | all-to-all | bytes 1638400 | tf_op jit(solution)/shard_map/all_to_all | solution.py:53
  323.2 5.0 reshape.148
  334.7 4.7 copy.103
  339.4 5.1 reshape.135
  344.5 25.6 %all_to_all.131 = bf16[4,2,51200]{2,1,0:T(2,128)(2,1)} all-to-all(bf16[4,2,51200]{2,1,0:T(2,128)(2,1)} %reshape.135), channel_id=1, replica_groups=mesh['rep'=8,'tp'=4] {'tp'}, dimensions={0} | all-to-all | bytes 1638400 | tf_op jit(solution)/shard_map/all_to_all | solution.py:54
  370.2 5.0 reshape.136
  392.4 8.8 fusion.26
  401.2 29.3 %all-gather.21.cloned.1.call-done = bf16[2,1280,1280]{2,1,0:T(8,128)(2,1)} async-done(((bf16[2,160,1280]{2,1,0:T(8,128)(2,1)}), bf16[2,1280,1280]{2,1,0:T(8,128)(2,1)}) %all-gather.21.cloned.1.call-update) | async-done | bytes 6553616 | tf_op jit(solution)/shard_map/all_gather | solution.py:62
  430.5 48.4 %all-gather.23.cloned.1.call-done = bf16[2,1280,1280]{2,1,0:T(8,128)(2,1)} async-done(((bf16[2,160,1280]{2,1,0:T(8,128)(2,1)}), bf16[2,1280,1280]{2,1,0:T(8,128)(2,1)}) %all-gather.23.cloned.1.call-update) | async-done | bytes 6553616 | tf_op jit(solution)/shard_map/all_gather | solution.py:63
  478.9 23.3 %convolution_convert_fusion.2 = bf16[1024,1280]{1,0:T(8,128)(2,1)} fusion(bf16[2,1280,1280]{2,1,0:T(8,128)(2,1)} %all-gather.23.cloned.1.call-done, f32[1024,1280]{1,0:T(8,128)} %fusion.26, bf16[1024,1280]{1,0:T(8,128)(2,1)} %multiply_convert_fusion.2, bf16[2,1280,1280]{2,1,0:T(8,128)(2,1)} %all-gather.21.cloned.1.call-done), kind=kOutput, calls=%fused_computation.57 | convolution fusion | flops 6798704640 | bytes 17039360 | tf_op jit(solution)/shard_map/dot_general | solution.py:88
  502.3 104.2 %all-reduce.7.cloned.1.call-done = bf16[1024,1280]{1,0:T(8,128)(2,1)} async-done(((bf16[1024,1280]{1,0:T(8,128)(2,1)}), bf16[1024,1280]{1,0:T(8,128)(2,1)}) %all-reduce.7.cloned.1.call-update) | async-done | bytes 2621456 | tf_op jit(solution)/shard_map/psum | solution.py:124
  637.8 103.2 %all-reduce.9.cloned.1.call-done = bf16[1024,1280]{1,0:T(8,128)(2,1)} async-done(((bf16[1024,1280]{1,0:T(8,128)(2,1)}), bf16[1024,1280]{1,0:T(8,128)(2,1)}) %all-reduce.9.cloned.1.call-update) | async-done | bytes 2621456 | tf_op jit(solution)/shard_map/psum | solution.py:124
  747.2 7.9 fusion.25
  755.1 24.4 %convolution_convert_fusion = bf16[1024,1280]{1,0:T(8,128)(2,1)} fusion(bf16[2,1280,1280]{2,1,0:T(8,128)(2,1)} %all-gather.23.cloned.1.call-done, f32[1024,1280]{1,0:T(8,128)} %fusion.25, bf16[2,1280,1280]{2,1,0:T(8,128)(2,1)} %all-gather.21.cloned.1.call-done, f32[1024,1280]{1,0:T(8,128)} %copy-done.5, f32[1280]{0:T(1024)S(1)} %get-tuple-element.5, ...), kind=kOutput, calls=%fused_computation.55 | convolution fusion | flops 6803947520 | bytes 19674112 | tf_op jit(solution)/shard_map/dot_general | solution.py:88
  779.4 103.2 %all-reduce.11.cloned.1.call-done = bf16[1024,1280]{1,0:T(8,128)(2,1)} async-done(((bf16[1024,1280]{1,0:T(8,128)(2,1)}), bf16[1024,1280]{1,0:T(8,128)(2,1)}) %all-reduce.11.cloned.1.call-update) | async-done | bytes 2621456 | tf_op jit(solution)/shard_map/psum | solution.py:124
  (138 shorter events, 116.2 us)
Async XLA Ops:
  6.5 85.3 %copy-start = (f32[32,1280]{1,0:T(8,128)S(1)}, f32[32,1280]{1,0:T(8,128)}, u32[]{:S(2)}) copy-start(f32[32,1280]{1,0:T(8,128)} %param.16) | copy-start | bytes 491524
  6.5 19.6 %copy-start.6 = (bf16[2,40,1280]{2,1,0:T(8,128)(2,1)S(1)}, bf16[2,40,1280]{2,1,0:T(8,128)(2,1)}, u32[]{:S(2)}) copy-start(bf16[2,40,1280]{2,1,0:T(8,128)(2,1)} %param.20) | copy-start | bytes 614404
  6.5 43.5 %copy-start.7 = (bf16[2,40,1280]{2,1,0:T(8,128)(2,1)S(1)}, bf16[2,40,1280]{2,1,0:T(8,128)(2,1)}, u32[]{:S(2)}) copy-start(bf16[2,40,1280]{2,1,0:T(8,128)(2,1)} %param.21) | copy-start | bytes 614404
  6.5 85.3 %all-gather.9.cloned.1.call-start = ((), (), s32[]{:S(2)}) async-start(), calls=%async_computation.7 | async-start | bytes 3276800 | tf_op jit(solution)/shard_map/all_gather | solution.py:117
  7.3 97.5 %all-gather.13.cloned.1.call-start = ((), (), s32[]{:S(2)}) async-start(), calls=%async_computation.9 | async-start | bytes 2211840 | tf_op jit(solution)/shard_map/all_gather | solution.py:57
  24.6 44.4 %copy-start.8 = (bf16[2,40,1280]{2,1,0:T(8,128)(2,1)S(1)}, bf16[2,40,1280]{2,1,0:T(8,128)(2,1)}, u32[]{:S(2)}) copy-start(bf16[2,40,1280]{2,1,0:T(8,128)(2,1)} %param.22) | copy-start | bytes 614404
  26.1 107.8 %all-gather.15.cloned.1.call-start = ((), (), s32[]{:S(2)}) async-start(), calls=%async_computation.10 | async-start | bytes 2211840 | tf_op jit(solution)/shard_map/all_gather | solution.py:58
  26.7 48.7 %copy-start.12 = (s32[4]{0:T(128)S(1)}, s32[4]{0:T(128)}, u32[]{:S(2)}) copy-start(s32[4]{0:T(128)} %param.15) | copy-start | bytes 52
  26.7 48.8 %copy-start.11 = (s32[4,4]{1,0:T(4,128)S(1)}, s32[4,4]{1,0:T(4,128)}, u32[]{:S(2)}) copy-start(s32[4,4]{1,0:T(4,128)} %param.14) | copy-start | bytes 196
  26.7 48.9 %copy-start.9 = (f32[2,1280]{1,0:T(2,128)S(1)}, f32[2,1280]{1,0:T(2,128)}, u32[]{:S(2)}) copy-start(f32[2,1280]{1,0:T(2,128)} %param.17) | copy-start | bytes 30724
  50.0 112.9 %all-gather.11.cloned.1.call-start = ((), (), s32[]{:S(2)}) async-start(), calls=%async_computation.8 | async-start | bytes 2211840 | tf_op jit(solution)/shard_map/all_gather | solution.py:59
  71.3 15.0 %all-to-all-start.3 = ((bf16[4,2,12800]{2,1,0:T(2,128)(2,1)}), bf16[4,2,12800]{2,1,0:T(2,128)(2,1)}, u32[]{:S(2)}, u32[]{:S(2)}) async-start(bf16[4,2,12800]{2,1,0:T(2,128)(2,1)} %reshape.143), calls=%async_computation.3 | async-start | bytes 409600 | tf_op jit(solution)/shard_map/all_to_all | solution.py:51
  75.3 116.7 %all-gather.17.cloned.1.call-start = ((), (), s32[]{:S(2)}) async-start(), calls=%async_computation.11 | async-start | bytes 2211840 | tf_op jit(solution)/shard_map/all_gather | solution.py:60
  91.6 290.2 %all-reduce.5.cloned.1.call-start = ((), (), s32[]{:S(2)}) async-start(), calls=%async_computation.12 | async-start | bytes 5242880 | tf_op jit(solution)/shard_map/psum | solution.py:124
  97.0 2.3 copy-start.2
  196.3 196.1 %all-gather.19.cloned.1.call-start = ((), (), s32[]{:S(2)}) async-start(), calls=%async_computation.13 | async-start | bytes 7372800 | tf_op jit(solution)/shard_map/all_gather | solution.py:61
  265.8 164.7 %all-gather.21.cloned.1.call-start = ((), (), s32[]{:S(2)}) async-start(), calls=%async_computation.14 | async-start | bytes 7372800 | tf_op jit(solution)/shard_map/all_gather | solution.py:62
  334.7 144.3 %all-gather.23.cloned.1.call-start = ((), (), s32[]{:S(2)}) async-start(), calls=%async_computation.15 | async-start | bytes 7372800 | tf_op jit(solution)/shard_map/all_gather | solution.py:63
  344.5 37.2 %copy-start.10 = (f32[2,1280]{1,0:T(2,128)S(1)}, f32[2,1280]{1,0:T(2,128)}, u32[]{:S(2)}) copy-start(f32[2,1280]{1,0:T(2,128)} %param.18) | copy-start | bytes 30724
  381.6 224.9 %all-reduce.7.cloned.1.call-start = ((), (), s32[]{:S(2)}) async-start(), calls=%async_computation.16 | async-start | bytes 5242880 | tf_op jit(solution)/shard_map/psum | solution.py:124
  381.8 4.1 copy-start.4
  381.8 7.7 slice-start
  385.8 3.7 slice-start.1
  502.3 238.7 %all-reduce.9.cloned.1.call-start = ((), (), s32[]{:S(2)}) async-start(), calls=%async_computation.17 | async-start | bytes 5242880 | tf_op jit(solution)/shard_map/psum | solution.py:124
  610.7 2.3 copy-start.3
  611.4 2.7 copy-start.13
  631.8 2.7 copy-start.14
  637.8 244.9 %all-reduce.11.cloned.1.call-start = ((), (), s32[]{:S(2)}) async-start(), calls=%async_computation.18 | async-start | bytes 5242880 | tf_op jit(solution)/shard_map/psum | solution.py:124
  744.9 2.3 copy-start.5
  755.0 130.1 %copy-start.1 = (f32[32,1280]{1,0:T(8,128)S(1)}, f32[32,1280]{1,0:T(8,128)}, u32[]{:S(2)}) copy-start(f32[32,1280]{1,0:T(8,128)} %param.16) | copy-start | bytes 491524
Sparse Core Ops, SparseCore 0:
  8.9 66.1 all-gather.8
  77.0 27.7 all-gather.12
  106.7 27.2 all-gather.14
  135.7 27.2 all-gather.10
  164.7 27.2 all-gather.16
  196.4 138.2 all-reduce.4
  336.6 45.3 all-gather.18
  384.0 46.4 all-gather.20
  432.4 46.4 all-gather.22
  502.4 104.0 all-reduce.6
  637.9 103.0 all-reduce.8
  779.6 103.0 all-reduce.10
where the time goes:
time: 902 us; the launch traced here: 892 us
  waiting for transfers between devices  460 us (51%)
  blocking collectives  169 us (19%)
  matrix products  105 us (12%)
  local copies, waits for them, and re-layouts  103 us (11%)
  other arithmetic  35.2 us (4%)
  between operations  14.7 us (2%)
    psum x4, waiting for transfers between devices, total_terms(): lax.psum(partial_value.astype(jnp.bfloat16), 'tp').astype(jnp.float32)  311 us
    unnamed x57, local copies, waits for them, and re-layouts  62.7 us
    dot_general x4, matrix products, out_terms(): lax.dot_general(mixed_rows, weight, (((1,), (1,)), ((), ())), preferred_e...  55.2 us
    all_gather x1, waiting for transfers between devices, reshard(): lax.all_gather(owned[6], 'rep', axis=1, tiled=True)  48.4 us
    all_to_all x1, blocking collectives, reshard(): lax.all_to_all(weights[4], 'tp', split_axis=2, concat_axis=1, tiled=True)  47.9 us
    all_to_all x1, blocking collectives, reshard(): lax.all_to_all(weights[5], 'tp', split_axis=2, concat_axis=1, tiled=True)  47.5 us
    all_gather x1, waiting for transfers between devices, reshard(): lax.all_gather(owned[5], 'rep', axis=1, tiled=True)  29.3 us
    all_to_all x1, blocking collectives, reshard(): lax.all_to_all(weights[6], 'tp', split_axis=2, concat_axis=1, tiled=True)  25.6 us
  transfers between devices with their start and end apart: 13, of which 9 were waited for; matrix products, arithmetic and copies ran while one was open for 16% of the time, Pallas kernels for 0%

commit v1 on v0

--- a/solution.py
+++ b/solution.py
@@ -121,7 +121,9 @@
     )
 
     def total_terms(partial_value):
-        return lax.psum(partial_value.astype(jnp.bfloat16), "tp").astype(jnp.float32)
+        return jnp.sum(lax.all_gather(partial_value.astype(jnp.bfloat16), "tp"), axis=0).astype(
+            jnp.float32
+        )
 
     for layer_index in range(LAYERS):
         query_here = query_w[layer_index]

time: 902 us -> 1260 us (1.40)
  waiting for transfers between devices: 460 us -> 768 us
  other arithmetic: 35.2 us -> 63 us
  blocking collectives: 169 us -> 190 us
    all_gather x0 -> x4, waiting for transfers between devices: none -> 579 us  [total_terms(): lax.all_gather(partial_value.astype(jnp.bfloat16), 'tp')]
    psum x4 -> x0, waiting for transfers between devices: 311 us -> none  [total_terms(): lax.psum(partial_value.astype(jnp.bfloat16), 'tp').astype(jnp.float32)]
    reduce_sum x0 -> x4, other arithmetic: none -> 29.6 us  [total_terms(): jnp.sum(lax.all_gather(partial_value.astype(jnp.bfloat16), 'tp'), axis=0)]
    all_gather x1, waiting for transfers between devices: 0.02 us -> 29.6 us  [reshard(): lax.all_gather(owned[4], 'rep', axis=1, tiled=True)]
    all_to_all x1, blocking collectives: 25.6 us -> 48.1 us  [reshard(): lax.all_to_all(weights[6], 'tp', split_axis=2, concat_axis=1, tiled=True)]
    unnamed x57 -> x55, local copies, waits for them, and re-layouts: 62.7 us -> 62.7 us
  transfers between devices with their start and end apart: 13 -> 13, of which waited for: 9 -> 11; matrix products, arithmetic and copies ran while one was open for 16% -> 12% of each run, Pallas kernels for 0% -> 0%
where the time goes in v1:
time: 1260 us; the launch traced here: 1250 us
  waiting for transfers between devices  768 us (61%)
  blocking collectives  190 us (15%)
  matrix products  105 us (8%)
  local copies, waits for them, and re-layouts  103 us (8%)
  other arithmetic  63 us (5%)
  between operations  14.6 us (1%)
    all_gather x4, waiting for transfers between devices, total_terms(): lax.all_gather(partial_value.astype(jnp.bfloat16), 'tp')  579 us
    unnamed x55, local copies, waits for them, and re-layouts  62.7 us
    dot_general x4, matrix products, out_terms(): lax.dot_general(mixed_rows, weight, (((1,), (1,)), ((), ())), preferred_e...  55.3 us
    all_gather x1, waiting for transfers between devices, reshard(): lax.all_gather(owned[6], 'rep', axis=1, tiled=True)  48.4 us
    all_to_all x1, blocking collectives, reshard(): lax.all_to_all(weights[6], 'tp', split_axis=2, concat_axis=1, tiled=True)  48.1 us
    all_to_all x1, blocking collectives, reshard(): lax.all_to_all(weights[5], 'tp', split_axis=2, concat_axis=1, tiled=True)  48.1 us
    all_to_all x1, blocking collectives, reshard(): lax.all_to_all(weights[4], 'tp', split_axis=2, concat_axis=1, tiled=True)  45.1 us
    all_gather x1, waiting for transfers between devices, reshard(): lax.all_gather(owned[5], 'rep', axis=1, tiled=True)  39.9 us
  transfers between devices with their start and end apart: 13, of which 11 were waited for; matrix products, arithmetic and copies ran while one was open for 12% of the time, Pallas kernels for 0%

profile of v1, /device:TPU:0, one launch (start us, length us, event | category | flops | bytes accessed | tf_op | source)
XLA Modules:
  0.0 1248.9 jit_solution(11775497687756586552)
XLA Ops:
  9.8 13.8 %all_to_all.126 = bf16[4,2,12800]{2,1,0:T(2,128)(2,1)S(1)} all-to-all(bf16[4,2,12800]{2,1,0:T(2,128)(2,1)S(1)} %reshape.143), channel_id=1, replica_groups=mesh['rep'=8,'tp'=4] {'tp'}, dimensions={0} | all-to-all | bytes 409600 | tf_op jit(solution)/shard_map/all_to_all | solution.py:48
  27.8 19.7 %all_to_all.127 = bf16[4,2,12800]{2,1,0:T(2,128)(2,1)S(1)} all-to-all(bf16[4,2,12800]{2,1,0:T(2,128)(2,1)S(1)} %reshape.141), channel_id=1, replica_groups=mesh['rep'=8,'tp'=4] {'tp'}, dimensions={0} | all-to-all | bytes 409600 | tf_op jit(solution)/shard_map/all_to_all | solution.py:49
  51.6 14.9 %all_to_all.128 = bf16[4,2,12800]{2,1,0:T(2,128)(2,1)S(1)} all-to-all(bf16[4,2,12800]{2,1,0:T(2,128)(2,1)S(1)} %reshape.145), channel_id=1, replica_groups=mesh['rep'=8,'tp'=4] {'tp'}, dimensions={0} | all-to-all | bytes 409600 | tf_op jit(solution)/shard_map/all_to_all | solution.py:50
  75.7 10.5 multiply_cosine_fusion
  91.8 5.1 fusion.139
  109.7 24.3 %all-gather.23.cloned.1.call-done = bf16[2,1280,320]{2,1,0:T(8,128)(2,1)} async-done(((bf16[2,160,320]{2,1,0:T(8,128)(2,1)}), bf16[2,1280,320]{2,1,0:T(8,128)(2,1)}) %all-gather.23.cloned.1.call-update) | async-done | bytes 1638416 | tf_op jit(solution)/shard_map/all_gather | solution.py:58
  139.5 23.5 %all-gather.19.cloned.1.call-done = bf16[2,1280,320]{2,1,0:T(8,128)(2,1)} async-done(((bf16[2,160,320]{2,1,0:T(8,128)(2,1)}), bf16[2,1280,320]{2,1,0:T(8,128)(2,1)}) %all-gather.19.cloned.1.call-update) | async-done | bytes 1638416 | tf_op jit(solution)/shard_map/all_gather | solution.py:59
  173.8 18.1 %all-gather.25.cloned.1.call-done = bf16[2,1280,320]{2,1,0:T(8,128)(2,1)} async-done(((bf16[2,160,320]{2,1,0:T(8,128)(2,1)}), bf16[2,1280,320]{2,1,0:T(8,128)(2,1)}) %all-gather.25.cloned.1.call-update) | async-done | bytes 1638416 | tf_op jit(solution)/shard_map/all_gather | solution.py:60
  201.5 5.1 reshape.149
  206.6 45.1 %all_to_all.129 = bf16[4,2,51200]{2,1,0:T(2,128)(2,1)} all-to-all(bf16[4,2,51200]{2,1,0:T(2,128)(2,1)} %reshape.149), channel_id=1, replica_groups=mesh['rep'=8,'tp'=4] {'tp'}, dimensions={0} | all-to-all | bytes 1638400 | tf_op jit(solution)/shard_map/all_to_all | solution.py:52
  251.7 5.0 reshape.150
  268.0 5.1 reshape.151
  273.1 48.1 %all_to_all.130 = bf16[4,2,51200]{2,1,0:T(2,128)(2,1)} all-to-all(bf16[4,2,51200]{2,1,0:T(2,128)(2,1)} %reshape.151), channel_id=1, replica_groups=mesh['rep'=8,'tp'=4] {'tp'}, dimensions={0} | all-to-all | bytes 1638400 | tf_op jit(solution)/shard_map/all_to_all | solution.py:53
  321.2 5.0 reshape.152
  337.5 5.1 reshape.139
  342.6 48.1 %all_to_all.131 = bf16[4,2,51200]{2,1,0:T(2,128)(2,1)} all-to-all(bf16[4,2,51200]{2,1,0:T(2,128)(2,1)} %reshape.139), channel_id=1, replica_groups=mesh['rep'=8,'tp'=4] {'tp'}, dimensions={0} | all-to-all | bytes 1638400 | tf_op jit(solution)/shard_map/all_to_all | solution.py:54
  390.7 5.0 reshape.140
  402.3 30.5 %all-gather.33.cloned.1.call-done = bf16[4096,1280]{1,0:T(8,128)(2,1)} async-done(((bf16[1024,1280]{1,0:T(8,128)(2,1)}), bf16[4096,1280]{1,0:T(8,128)(2,1)}) %all-gather.33.cloned.1.call-update) | async-done | bytes 10485776 | tf_op jit(solution)/shard_map/all_gather | solution.py:124
  432.7 7.3 reduce_sum.161
  449.8 29.6 %all-gather.27.cloned.1.call-done = bf16[2,1280,1280]{2,1,0:T(8,128)(2,1)} async-done(((bf16[2,160,1280]{2,1,0:T(8,128)(2,1)}), bf16[2,1280,1280]{2,1,0:T(8,128)(2,1)}) %all-gather.27.cloned.1.call-update) | async-done | bytes 6553616 | tf_op jit(solution)/shard_map/all_gather | solution.py:61
  479.3 8.6 fusion.26
  487.9 39.9 %all-gather.29.cloned.1.call-done = bf16[2,1280,1280]{2,1,0:T(8,128)(2,1)} async-done(((bf16[2,160,1280]{2,1,0:T(8,128)(2,1)}), bf16[2,1280,1280]{2,1,0:T(8,128)(2,1)}) %all-gather.29.cloned.1.call-update) | async-done | bytes 6553616 | tf_op jit(solution)/shard_map/all_gather | solution.py:62
  527.7 48.4 %all-gather.31.cloned.1.call-done = bf16[2,1280,1280]{2,1,0:T(8,128)(2,1)} async-done(((bf16[2,160,1280]{2,1,0:T(8,128)(2,1)}), bf16[2,1280,1280]{2,1,0:T(8,128)(2,1)}) %all-gather.31.cloned.1.call-update) | async-done | bytes 6553616 | tf_op jit(solution)/shard_map/all_gather | solution.py:63
  576.2 23.6 %convolution_convert_fusion.2 = bf16[1024,1280]{1,0:T(8,128)(2,1)} fusion(bf16[2,1280,1280]{2,1,0:T(8,128)(2,1)} %all-gather.31.cloned.1.call-done, f32[1024,1280]{1,0:T(8,128)} %fusion.26, bf16[1024,1280]{1,0:T(8,128)(2,1)} %multiply_convert_fusion.2, bf16[2,1280,1280]{2,1,0:T(8,128)(2,1)} %all-gather.29.cloned.1.call-done), kind=kOutput, calls=%fused_computation.57 | convolution fusion | flops 6798704640 | bytes 17039360 | tf_op jit(solution)/shard_map/dot_general | solution.py:88
  599.9 184.0 %all-gather.35.cloned.1.call-done = bf16[4096,1280]{1,0:T(8,128)(2,1)} async-done(((bf16[1024,1280]{1,0:T(8,128)(2,1)}), bf16[4096,1280]{1,0:T(8,128)(2,1)}) %all-gather.35.cloned.1.call-update) | async-done | bytes 10485776 | tf_op jit(solution)/shard_map/all_gather | solution.py:124
  783.9 7.8 reduce_sum.164
  822.9 182.2 %all-gather.37.cloned.1.call-done = bf16[4096,1280]{1,0:T(8,128)(2,1)} async-done(((bf16[1024,1280]{1,0:T(8,128)(2,1)}), bf16[4096,1280]{1,0:T(8,128)(2,1)}) %all-gather.37.cloned.1.call-update) | async-done | bytes 10485776 | tf_op jit(solution)/shard_map/all_gather | solution.py:124
  1005.1 7.3 reduce_sum.168
  1017.7 7.8 fusion.25
  1025.5 24.3 %convolution_convert_fusion = bf16[1024,1280]{1,0:T(8,128)(2,1)} fusion(bf16[2,1280,1280]{2,1,0:T(8,128)(2,1)} %all-gather.31.cloned.1.call-done, f32[1024,1280]{1,0:T(8,128)} %fusion.25, bf16[2,1280,1280]{2,1,0:T(8,128)(2,1)} %all-gather.29.cloned.1.call-done, f32[1024,1280]{1,0:T(8,128)} %copy-done.4, f32[1280]{0:T(1024)S(1)} %get-tuple-element.5, ...), kind=kOutput, calls=%fused_computation.55 | convolution fusion | flops 6803947520 | bytes 19674112 | tf_op jit(solution)/shard_map/dot_general | solution.py:88
  1049.8 182.2 %all-gather.39.cloned.1.call-done = bf16[4096,1280]{1,0:T(8,128)(2,1)} async-done(((bf16[1024,1280]{1,0:T(8,128)(2,1)}), bf16[4096,1280]{1,0:T(8,128)(2,1)}) %all-gather.39.cloned.1.call-update) | async-done | bytes 10485776 | tf_op jit(solution)/shard_map/all_gather | solution.py:124
  1232.0 7.3 reduce_sum.171
  (140 shorter events, 142.1 us)
Async XLA Ops:
  6.5 85.3 %copy-start = (f32[32,1280]{1,0:T(8,128)S(1)}, f32[32,1280]{1,0:T(8,128)}, u32[]{:S(2)}) copy-start(f32[32,1280]{1,0:T(8,128)} %param.16) | copy-start | bytes 491524
  6.5 19.6 %copy-start.5 = (bf16[2,40,1280]{2,1,0:T(8,128)(2,1)S(1)}, bf16[2,40,1280]{2,1,0:T(8,128)(2,1)}, u32[]{:S(2)}) copy-start(bf16[2,40,1280]{2,1,0:T(8,128)(2,1)} %param.20) | copy-start | bytes 614404
  6.5 43.5 %copy-start.6 = (bf16[2,40,1280]{2,1,0:T(8,128)(2,1)S(1)}, bf16[2,40,1280]{2,1,0:T(8,128)(2,1)}, u32[]{:S(2)}) copy-start(bf16[2,40,1280]{2,1,0:T(8,128)(2,1)} %param.21) | copy-start | bytes 614404
  6.5 85.2 %all-gather.17.cloned.1.call-start = ((), (), s32[]{:S(2)}) async-start(), calls=%async_computation.7 | async-start | bytes 3276800 | tf_op jit(solution)/shard_map/all_gather | solution.py:117
  7.3 97.5 %all-gather.21.cloned.1.call-start = ((), (), s32[]{:S(2)}) async-start(), calls=%async_computation.9 | async-start | bytes 2211840 | tf_op jit(solution)/shard_map/all_gather | solution.py:57
  24.6 44.3 %copy-start.7 = (bf16[2,40,1280]{2,1,0:T(8,128)(2,1)S(1)}, bf16[2,40,1280]{2,1,0:T(8,128)(2,1)}, u32[]{:S(2)}) copy-start(bf16[2,40,1280]{2,1,0:T(8,128)(2,1)} %param.22) | copy-start | bytes 614404
  26.1 107.9 %all-gather.23.cloned.1.call-start = ((), (), s32[]{:S(2)}) async-start(), calls=%async_computation.10 | async-start | bytes 2211840 | tf_op jit(solution)/shard_map/all_gather | solution.py:58
  26.7 48.7 %copy-start.11 = (s32[4]{0:T(128)S(1)}, s32[4]{0:T(128)}, u32[]{:S(2)}) copy-start(s32[4]{0:T(128)} %param.15) | copy-start | bytes 52
  26.7 48.7 %copy-start.10 = (s32[4,4]{1,0:T(4,128)S(1)}, s32[4,4]{1,0:T(4,128)}, u32[]{:S(2)}) copy-start(s32[4,4]{1,0:T(4,128)} %param.14) | copy-start | bytes 196
  26.7 48.8 %copy-start.8 = (f32[2,1280]{1,0:T(2,128)S(1)}, f32[2,1280]{1,0:T(2,128)}, u32[]{:S(2)}) copy-start(f32[2,1280]{1,0:T(2,128)} %param.17) | copy-start | bytes 30724
  50.0 113.0 %all-gather.19.cloned.1.call-start = ((), (), s32[]{:S(2)}) async-start(), calls=%async_computation.8 | async-start | bytes 2211840 | tf_op jit(solution)/shard_map/all_gather | solution.py:59
  71.2 14.9 %all-to-all-start.3 = ((bf16[4,2,12800]{2,1,0:T(2,128)(2,1)}), bf16[4,2,12800]{2,1,0:T(2,128)(2,1)}, u32[]{:S(2)}, u32[]{:S(2)}) async-start(bf16[4,2,12800]{2,1,0:T(2,128)(2,1)} %reshape.147), calls=%async_computation.3 | async-start | bytes 409600 | tf_op jit(solution)/shard_map/all_to_all | solution.py:51
  75.2 116.7 %all-gather.25.cloned.1.call-start = ((), (), s32[]{:S(2)}) async-start(), calls=%async_computation.11 | async-start | bytes 2211840 | tf_op jit(solution)/shard_map/all_gather | solution.py:60
  91.5 341.2 %all-gather.33.cloned.1.call-start = ((), (), s32[]{:S(2)}) async-start(), calls=%async_computation.15 | async-start | bytes 13107200 | tf_op jit(solution)/shard_map/all_gather | solution.py:124
  96.9 2.3 copy-start.2
  196.3 283.0 %all-gather.27.cloned.1.call-start = ((), (), s32[]{:S(2)}) async-start(), calls=%async_computation.12 | async-start | bytes 7372800 | tf_op jit(solution)/shard_map/all_gather | solution.py:61
  263.3 264.5 %all-gather.29.cloned.1.call-start = ((), (), s32[]{:S(2)}) async-start(), calls=%async_computation.13 | async-start | bytes 7372800 | tf_op jit(solution)/shard_map/all_gather | solution.py:62
  332.7 243.5 %all-gather.31.cloned.1.call-start = ((), (), s32[]{:S(2)}) async-start(), calls=%async_computation.14 | async-start | bytes 7372800 | tf_op jit(solution)/shard_map/all_gather | solution.py:63
  342.6 59.6 %copy-start.9 = (f32[2,1280]{1,0:T(2,128)S(1)}, f32[2,1280]{1,0:T(2,128)}, u32[]{:S(2)}) copy-start(f32[2,1280]{1,0:T(2,128)} %param.18) | copy-start | bytes 30724
  402.2 381.7 %all-gather.35.cloned.1.call-start = ((), (), s32[]{:S(2)}) async-start(), calls=%async_computation.16 | async-start | bytes 13107200 | tf_op jit(solution)/shard_map/all_gather | solution.py:124
  440.0 7.1 slice-start
  443.6 3.6 slice-start.1
  599.8 405.2 %all-gather.37.cloned.1.call-start = ((), (), s32[]{:S(2)}) async-start(), calls=%async_computation.17 | async-start | bytes 13107200 | tf_op jit(solution)/shard_map/all_gather | solution.py:124
  795.9 2.3 copy-start.3
  796.5 2.7 copy-start.12
  816.9 2.7 copy-start.13
  822.8 409.2 %all-gather.39.cloned.1.call-start = ((), (), s32[]{:S(2)}) async-start(), calls=%async_computation.18 | async-start | bytes 13107200 | tf_op jit(solution)/shard_map/all_gather | solution.py:124
  1015.4 2.3 copy-start.4
  1232.0 9.6 copy-start.1
Sparse Core Ops, SparseCore 0:
  8.9 66.0 all-gather.16
  76.9 27.7 all-gather.20
  106.7 27.2 all-gather.22
  135.7 27.2 all-gather.18
  164.7 27.2 all-gather.24
  196.4 236.2 all-gather.32
  434.6 44.6 all-gather.26
  481.2 46.4 all-gather.28
  529.6 46.4 all-gather.30
  600.0 183.8 all-gather.34
  822.9 182.0 all-gather.36
  1049.9 182.0 all-gather.38
